TPU v7x, 32 devices: a whole 2x2x4 slice. The times are simulated.
32 devices in a mesh: occ: 2 (over x), vir: 4 (over z), aux: 4 (over y, core).
Axes of the slice: x: 2, y: 2, z: 4, core: 2. Of those that a mesh axis runs over, the one named last changes fastest.
Arguments:
- amplitudes: bfloat16 [16, 1024, 1024], P('occ', 'vir'), may hold values from -6 to 6
- pair_mask: int32 [16, 8, 8], P('occ', 'vir'), may hold values 0 or 1
- left_factor: bfloat16 [32, 1024, 4096], P(None, 'vir', 'aux'), may hold values from -0.0390625 to 0.0390625
- left_mask: int32 [8, 32], P('vir', 'aux'), may hold values 0 or 1
- right_factor: bfloat16 [1024, 4, 4096], P(('occ', 'vir'), None, 'aux'), may hold values from -0.0390625 to 0.0390625
- right_mask: int32 [8, 32], P(None, 'aux'), may hold values 0 or 1
- residual_in: float32 [16, 4, 32], P('occ'), may hold values from -6 to 6
Outputs:
- updated: float32 [16, 4, 32], P('occ')
All inputs are finite; a program needn't handle non-finite values. No bound on the sum of `pair_mask` or of `left_mask` or of `right_mask` on one device may be relied on, other than what follows from the above.
Results may differ from a plain program's by a relative error of at most 0.0003.
Values may be sent and summed in bfloat16 or wider, within the bound.
A program may use at most 128 MiB of HBM per device.

v0:
```python
import jax
import jax.numpy as jnp
from jax import lax
from jax.sharding import PartitionSpec as P

TILE = 128


def expand_tiles(mask, width):
    return jnp.repeat(jnp.repeat(mask, width, axis=-2), width, axis=-1)


def local(amplitudes, pair_mask, left_factor, left_mask, right_factor, right_mask, residual_in):
    pairs_here, cols_here, virt_all = amplitudes.shape
    rows_here, block_b, aux_here = right_factor.shape
    tau = amplitudes * expand_tiles(pair_mask, TILE).astype(jnp.bfloat16)
    left = left_factor * expand_tiles(left_mask, TILE).astype(jnp.bfloat16)[None, :, :]
    tiles_all = right_mask.shape[0]
    aux_mask = jnp.repeat(right_mask, TILE, axis=1).astype(jnp.float32)
    row_start = lax.axis_index(("occ", "vir")) * rows_here
    row_tiles = (row_start + jnp.arange(rows_here, dtype=jnp.int32)) // TILE
    onehot = (row_tiles[:, None] == jnp.arange(tiles_all, dtype=jnp.int32)[None, :]).astype(
        jnp.float32
    )
    row_mask = jnp.dot(onehot, aux_mask, preferred_element_type=jnp.float32)
    right = right_factor * row_mask.astype(jnp.bfloat16)[:, None, :]
    right_whole = lax.all_gather(right, ("occ", "vir"), axis=0, tiled=True)
    tau_flat = tau.reshape(pairs_here * cols_here, virt_all)
    left_wide = left.astype(jnp.float32)
    columns = []
    for index_b in range(block_b):
        inner_b = jnp.dot(tau_flat, right_whole[:, index_b, :], preferred_element_type=jnp.float32)
        inner_b = inner_b.reshape(pairs_here, cols_here, aux_here)
        columns.append(
            jnp.einsum(
                "pcq,acq->pa",
                inner_b,
                left_wide,
                precision=lax.Precision.HIGHEST,
                preferred_element_type=jnp.float32,
            )
        )
    partial_sum = jnp.stack(columns, axis=1)
    total = lax.psum(partial_sum, ("vir", "aux"))
    return residual_in + total


def solution(mesh):
    return jax.shard_map(
        local,
        mesh=mesh,
        in_specs=(
            P("occ", "vir", None),
            P("occ", "vir", None),
            P(None, "vir", "aux"),
            P("vir", "aux"),
            P(("occ", "vir"), None, "aux"),
            P(None, "aux"),
            P("occ", None, None),
        ),
        out_specs=P("occ", None, None),
        check_vma=False,
    )
```

profile of v0, /device:TPU:0, one launch (start us, length us, event | category | flops | bytes accessed | tf_op | source)
XLA Modules:
  0.0 395.1 jit_solution(14707230647622306978)
XLA Ops:
  6.5 0.0 all-gather.2.cloned.1.call-start
  6.5 0.7 convert_element_type.41
  7.2 0.1 broadcast_bitcast_fusion
  7.3 0.3 convolution_convert_fusion
  7.6 0.0 copy-start.3
  7.6 3.0 copy_multiply_fusion
  10.6 0.0 all-gather.2.cloned.1.call-update
  10.6 0.7 convert_element_type.38
  11.3 0.1 broadcast_in_dim.19
  11.4 3.8 broadcast_in_dim.20
  15.2 7.4 %convert_element_type.40 = bf16[8,256,1024]{2,1,0:T(8,128)(2,1)} reshape(bf16[8,256,8,128]{3,2,1,0:T(8,128)(2,1)} %broadcast_in_dim.20) | data formatting | bytes 8388608 | tf_op jit(solution)/shard_map/convert_element_type | solution.py:16
  22.6 0.0 copy-done.3
  22.7 0.3 broadcast_in_dim.23
  23.0 0.1 copy.55
  23.1 7.9 %mul.25 = bf16[8,256,1024]{2,1,0:T(8,128)(2,1)} multiply(bf16[8,256,1024]{2,1,0:T(8,128)(2,1)} %param.7, bf16[8,256,1024]{2,1,0:T(8,128)(2,1)} %convert_element_type.40) | non-fusion elementwise | flops 2097152 | bytes 12582912 | tf_op jit(solution)/shard_map/mul | solution.py:16
  31.0 13.8 %broadcast_multiply_fusion = bf16[32,256,1024]{2,1,0:T(8,128)(2,1)} fusion(bf16[32,256,1024]{2,1,0:T(8,128)(2,1)} %param.9, bf16[256,1024]{1,0:T(8,128)(2,1)S(1)} %bitcast.45), kind=kLoop, calls=%fused_computation.8 | loop fusion | flops 8388608 | bytes 34078720 | tf_op jit(solution)/shard_map/mul | solution.py:17
  44.9 93.1 %all-gather.2.cloned.1.call-done = bf16[1024,4,1024]{2,0,1:T(8,128)(2,1)} async-done(((bf16[128,4,1024]{2,0,1:T(8,128)(2,1)}), bf16[1024,4,1024]{2,0,1:T(8,128)(2,1)}) %all-gather.2.cloned.1.call-update) | async-done | bytes 8388624 | tf_op jit(solution)/shard_map/all_gather | solution.py:27
  138.0 0.0 copy-start
  138.0 11.6 %fusion.14 = f32[8,256,1024]{2,0,1:T(8,128)} fusion(bf16[8,256,1024]{2,1,0:T(8,128)(2,1)} %mul.25, bf16[1024,4,1024]{2,0,1:T(8,128)(2,1)} %all-gather.2.cloned.1.call-done), kind=kOutput, calls=%fused_computation.15 | convolution fusion | flops 4294967296 | bytes 14680064 | tf_op jit(solution)/shard_map/dot_general | solution.py:32
  149.6 0.0 copy-done
  149.6 0.0 copy-start.1
  149.6 44.4 %fusion.16 = f32[8,1,32]{2,0,1:T(8,128)S(1)} fusion(f32[8,256,1024]{2,0,1:T(8,128)} %fusion.14, bf16[32,256,1024]{2,1,0:T(8,128)(2,1)S(1)} %copy-done), kind=kOutput, calls=%fused_computation.22 | convolution fusion | flops 805306368 | bytes 25166848 | tf_op jit(solution)/shard_map/pcq,acq->pa/dot_general | solution.py:35
  194.0 0.0 copy-done.1
  194.0 12.3 %fusion.12 = f32[8,256,1024]{2,0,1:T(8,128)} fusion(bf16[8,256,1024]{2,1,0:T(8,128)(2,1)S(1)} %copy-done.1, bf16[1024,4,1024]{2,0,1:T(8,128)(2,1)} %all-gather.2.cloned.1.call-done), kind=kOutput, calls=%fused_computation.13 | convolution fusion | flops 4294967296 | bytes 14680064 | tf_op jit(solution)/shard_map/dot_general | solution.py:32
  206.3 32.6 %fusion.19 = f32[8,1,32]{2,0,1:T(8,128)S(1)} fusion(f32[8,256,1024]{2,0,1:T(8,128)} %fusion.12, bf16[32,256,1024]{2,1,0:T(8,128)(2,1)S(1)} %copy-done), kind=kOutput, calls=%fused_computation.23 | convolution fusion | flops 805306368 | bytes 25166848 | tf_op jit(solution)/shard_map/pcq,acq->pa/dot_general | solution.py:35
  238.9 12.3 %fusion.10 = f32[8,256,1024]{2,0,1:T(8,128)} fusion(bf16[8,256,1024]{2,1,0:T(8,128)(2,1)S(1)} %copy-done.1, bf16[1024,4,1024]{2,0,1:T(8,128)(2,1)} %all-gather.2.cloned.1.call-done), kind=kOutput, calls=%fused_computation.11 | convolution fusion | flops 4294967296 | bytes 14680064 | tf_op jit(solution)/shard_map/dot_general | solution.py:32
  251.1 32.4 %fusion.22 = f32[8,1,32]{2,0,1:T(8,128)S(1)} fusion(f32[8,256,1024]{2,0,1:T(8,128)} %fusion.10, bf16[32,256,1024]{2,1,0:T(8,128)(2,1)S(1)} %copy-done), kind=kOutput, calls=%fused_computation.24 | convolution fusion | flops 805306368 | bytes 25166848 | tf_op jit(solution)/shard_map/pcq,acq->pa/dot_general | solution.py:35
  283.6 12.3 %fusion.8 = f32[8,256,1024]{2,0,1:T(8,128)} fusion(bf16[8,256,1024]{2,1,0:T(8,128)(2,1)S(1)} %copy-done.1, bf16[1024,4,1024]{2,0,1:T(8,128)(2,1)} %all-gather.2.cloned.1.call-done), kind=kOutput, calls=%fused_computation.9 | convolution fusion | flops 4294967296 | bytes 14680064 | tf_op jit(solution)/shard_map/dot_general | solution.py:32
  295.8 0.0 copy-start.2
  295.8 32.2 %fusion.25 = f32[8,1,32]{2,0,1:T(8,128)S(1)} fusion(f32[8,256,1024]{2,0,1:T(8,128)} %fusion.8, bf16[32,256,1024]{2,1,0:T(8,128)(2,1)S(1)} %copy-done), kind=kOutput, calls=%fused_computation.25 | convolution fusion | flops 805306368 | bytes 25166848 | tf_op jit(solution)/shard_map/pcq,acq->pa/dot_general | solution.py:35
  328.1 59.4 %psum.7 = f32[8,4,32]{2,0,1:T(8,128)S(1)} all-reduce(f32[8,4,32]{2,0,1:T(8,128)S(1)} %pad_maximum_fusion), channel_id=1, replica_groups=mesh['occ'=2,'vir'=4,'aux'=4] {'vir','aux'}, use_global_device_ids=true, to_apply=%region_0.1 | all-reduce | flops 1024 | bytes 8192 | tf_op jit(solution)/shard_map/psum | solution.py:44
  387.4 0.0 copy-done.2
  387.4 0.6 copy.20
  (5 shorter events, 0.0 us)
Async XLA Ops:
  6.5 131.4 %all-gather.2.cloned.1.call-start = ((), (), s32[]{:S(2)}) async-start(), calls=%async_computation | async-start | bytes 9437184 | tf_op jit(solution)/shard_map/all_gather | solution.py:27
  7.6 15.1 %copy-start.3 = (s32[2,8]{1,0:T(2,128)S(1)}, s32[2,8]{1,0:T(2,128)}, u32[]{:S(2)}) copy-start(s32[2,8]{1,0:T(2,128)} %param.10) | copy-start | bytes 196
  138.0 11.6 %copy-start = (bf16[32,256,1024]{2,1,0:T(8,128)(2,1)S(1)}, bf16[32,256,1024]{2,1,0:T(8,128)(2,1)}, u32[]{:S(2)}) copy-start(bf16[32,256,1024]{2,1,0:T(8,128)(2,1)} %broadcast_multiply_fusion) | copy-start | bytes 50331652
  149.6 44.4 %copy-start.1 = (bf16[8,256,1024]{2,1,0:T(8,128)(2,1)S(1)}, bf16[8,256,1024]{2,1,0:T(8,128)(2,1)}, u32[]{:S(2)}) copy-start(bf16[8,256,1024]{2,1,0:T(8,128)(2,1)} %mul.25) | copy-start | bytes 12582916
  295.8 91.6 %copy-start.2 = (f32[8,4,32]{2,1,0:T(4,128)S(1)}, f32[8,4,32]{2,1,0:T(4,128)}, u32[]{:S(2)}) copy-start(f32[8,4,32]{2,1,0:T(4,128)} %param.13) | copy-start | bytes 12292
Sparse Core Ops, SparseCore 0:
  10.7 127.1 all-gather.1
where the time goes:
time: 403 us; the launch traced here: 395 us
  matrix products  190 us (47%)
  waiting for transfers between devices  93.1 us (23%)
  blocking collectives  59.4 us (15%)
  other arithmetic  26.2 us (7%)
  between operations  13.6 us (3%)
  local copies, waits for them, and re-layouts  12.5 us (3%)
    dot_general x4, matrix products, local(): jnp.einsum('pcq,acq->pa', inner_b, left_wide, precision=lax.Precision.HIG...  142 us
    all_gather x1, waiting for transfers between devices, local(): right_whole = lax.all_gather(right, ('occ', 'vir'), axis=0, tiled=True)  93.1 us
    psum x1, blocking collectives, local(): total = lax.psum(partial_sum, ('vir', 'aux'))  59.4 us
    dot_general x4, matrix products, local(): jnp.dot(tau_flat, right_whole[:, index_b, :], preferred_element_type=jnp....  48.4 us
    mul x1, other arithmetic, local(): left_factor * expand_tiles(left_mask, TILE).astype(jnp.bfloat16)[None, :, :]  13.8 us
  transfers between devices with their start and end apart: 1, of which 1 were waited for; matrix products, arithmetic and copies ran while one was open for 9% of the time, Pallas kernels for 0%

commit v1 on v0

v1 whole, which is shorter than its diff:
```python
import functools

import jax
import jax.numpy as jnp
from jax import lax
from jax.experimental import pallas as pl
from jax.experimental.pallas import tpu as pltpu
from jax.sharding import PartitionSpec as P

TILE = 128
QC = 256
CC = 32
MESH = pl.DeviceIdType.MESH
F32 = jnp.float32
BF16 = jnp.bfloat16


def kernel(
    no, nv, na, pair_mask, left_mask, right_mask, amp_hbm, left_hbm, right_hbm, res,
    out, amp, left, rbuf, wr, tau, tsend, lhs2, rhs2, acc, part, parts,
    amp_sem, left_sem, own_sem, r_send, r_recv, t_send, t_recv, a_send, a_recv,
):
    occ, vir, aux = lax.axis_index("occ"), lax.axis_index("vir"), lax.axis_index("aux")
    pairs, cols, virt = amp.shape
    nq, _, bq = right_hbm.shape
    rows = rbuf.shape[2]
    block_b = bq // QC
    block_a = left.shape[0]
    cq, depth = tau.shape[3], tau.shape[4]
    pall = no * pairs
    steps = cols // CC
    subs = cq // CC
    groups = CC // 8

    def right_copy(u, n, down, own):
        src = right_hbm.at[n] if own else rbuf.at[u, n]
        return pltpu.make_async_remote_copy(
            src_ref=src,
            dst_ref=rbuf.at[u, n],
            send_sem=r_send.at[1 if down else 0, u, n],
            recv_sem=r_recv.at[u, n],
            device_id={"vir": vir - 1 if down else vir + 1},
            device_id_type=MESH,
        )

    def send_own(n):
        @pl.when(vir > 0)
        def _():
            right_copy(vir, n, True, True).start()

        @pl.when(vir < nv - 1)
        def _():
            right_copy(vir, n, False, True).start()

    def arrive(k, n, forwarded):
        for down in (True, False):
            u = vir + k if down else vir - k
            here = u < nv if down else u >= 0
            passes = vir > 0 if down else vir < nv - 1

            @pl.when(here & (passes if forwarded else jnp.logical_not(passes)))
            def _():
                right_copy(u, n, down, False).wait_recv()
                if forwarded:
                    right_copy(u, n, down, False).start()

    amp_copy = pltpu.make_async_copy(amp_hbm, amp, amp_sem)
    amp_copy.start()
    send_own(0)
    if nq > 1:
        send_own(1)
    own_copies = [
        pltpu.make_async_copy(right_hbm.at[n], rbuf.at[vir, n], own_sem.at[n]) for n in range(nq)
    ]
    for copy in own_copies:
        copy.start()

    def left_copy(n):
        return pltpu.make_async_copy(
            left_hbm.at[:, :, pl.ds(pl.multiple_of(n * QC, QC), QC)],
            left.at[:, :, pl.ds(pl.multiple_of(n * QC, QC), QC)],
            left_sem.at[n],
        )

    for n in range(nq):
        left_copy(n).start()
    amp_copy.wait()

    piece = min(cq, TILE)

    def masked(p, row, column):
        m = pair_mask[p, row // TILE, column // TILE].astype(F32)
        block = amp[
            p, pl.ds(pl.multiple_of(row, piece), piece), pl.ds(pl.multiple_of(column, TILE), TILE)
        ]
        return (block.astype(F32) * m).astype(BF16)

    def fill_send(p, carry):
        for k in range(1, no):
            base = lax.rem(occ + k, no) * depth
            for off in range(0, cq, piece):
                for col in range(0, depth, TILE):
                    tsend[k - 1, p, off : off + piece, col : col + TILE] = masked(
                        p, aux * cq + off, base + col
                    )
        return carry

    lax.fori_loop(0, pairs, fill_send, 0)

    def tau_copy(k, sem, q, src, device):
        slot = lax.rem(occ + k, no)
        return pltpu.make_async_remote_copy(
            src_ref=src,
            dst_ref=tau.at[slot, q],
            send_sem=t_send.at[k, sem],
            recv_sem=t_recv.at[slot, q],
            device_id=device,
            device_id_type=MESH,
        )

    def occ_copy(k):
        return pltpu.make_async_remote_copy(
            src_ref=tsend.at[k - 1],
            dst_ref=tau.at[occ, aux],
            send_sem=t_send.at[k, 0],
            recv_sem=t_recv.at[occ, aux],
            device_id={"occ": lax.rem(occ + k, no)},
            device_id_type=MESH,
        )

    acc[...] = jnp.zeros_like(acc)
    for k in range(1, no):
        occ_copy(k).start()

    def fill_own(i, carry):
        p, q = i // na, lax.rem(i, na)
        for off in range(0, cq, piece):
            for col in range(0, depth, TILE):
                tau[occ, q, p, off : off + piece, col : col + TILE] = masked(
                    p, q * cq + off, occ * depth + col
                )
        return carry

    lax.fori_loop(0, pairs * na, fill_own, 0)

    bits = []
    bit = na // 2
    while bit:
        bits.append(bit)
        bit //= 2
    have = [0]
    sent = 1
    tau_sends = [occ_copy(k) for k in range(1, no)]
    waves = list(range(1, nv))
    arrive(1, 0, True)
    for stage, bit in enumerate(bits):
        for k in range(1, no):
            for m in have if stage == 0 else have[len(have) // 2 :]:
                q = aux ^ m
                tau_copy(k, 0, q, tau.at[lax.rem(occ + k, no), q], {"aux": aux ^ bit}).wait_recv()
            for i, m in enumerate(have):
                q = aux ^ m
                copy = tau_copy(
                    k, sent + i, q, tau.at[lax.rem(occ + k, no), q], {"aux": aux ^ bit}
                )
                copy.start()
                tau_sends.append(copy)
        sent += len(have)
        have = have + [m ^ bit for m in have]
        if stage == 0:
            for k in waves[1:]:
                arrive(k, 0, True)
            if nq > 2:
                send_own(2)
    for k in range(1, no):
        for m in have[len(have) // 2 :] if bits else have:
            q = aux ^ m
            tau_copy(k, 0, q, tau.at[lax.rem(occ + k, no), q], {"occ": lax.rem(occ + k, no)}).wait_recv()
    for copy in own_copies:
        copy.wait()

    sub_rows = min(rows, TILE)
    lane = lax.broadcasted_iota(jnp.int32, (1, QC), 1)

    def step(it, carry):
        n = it // steps
        cs = lax.rem(it, steps)

        @pl.when(cs == 0)
        def _():
            for k in waves:
                arrive(k, n, False)
            left_copy(n).wait()
            for u in range(nv):
                for r in range(0, rows, sub_rows):
                    dt = (occ * depth + u * rows + r) // TILE
                    m = jnp.zeros((1, QC), F32)
                    for t in range(QC // TILE):
                        m = jnp.where(
                            lane // TILE == t, right_mask[dt, n * (QC // TILE) + t].astype(F32), m
                        )
                    for b in range(block_b):
                        x = rbuf[u, n, pl.ds(r, sub_rows), b * QC : (b + 1) * QC]
                        wr[u * rows + r : u * rows + r + sub_rows, b * QC : (b + 1) * QC] = (
                            x.astype(F32) * m
                        ).astype(BF16)

        for k in waves:
            @pl.when((cs == min(2 * k, steps - 1)) & (n + 1 < nq))
            def _():
                arrive(k, n + 1, True)
                if k == nv - 1:
                    @pl.when(n + 3 < nq)
                    def _():
                        send_own(n + 3)

        c0 = pl.multiple_of(cs * CC, CC)
        q0 = pl.multiple_of(n * QC, QC)
        lm = jnp.zeros((1, QC), F32)
        for t in range(QC // TILE):
            lm = jnp.where(
                lane // TILE == t, left_mask[cs * CC // TILE, n * (QC // TILE) + t].astype(F32), lm
            )
        w = left[:, pl.ds(c0, CC), pl.ds(q0, QC)].astype(F32) * lm[None]
        w = w.reshape(block_a, groups, 8, QC)
        for j in range(groups):
            rhs2[:, j * QC : (j + 1) * QC] = w[:, j].reshape(block_a * 8, QC).astype(BF16)
        q, s = cs // subs, lax.rem(cs, subs)
        t = tau[:, q, :, pl.ds(pl.multiple_of(s * CC, CC), CC), :].reshape(pall * CC, depth)
        half = pall * 8
        for b in range(block_b):
            inner = jnp.dot(t, wr[:, b * QC : (b + 1) * QC], preferred_element_type=F32)
            inner = inner.reshape(pall, groups, 8, QC)
            for j in range(groups):
                x = inner[:, j].reshape(half, QC)
                hi = x.astype(BF16)
                lo = (x - hi.astype(F32)).astype(BF16)
                lhs2[2 * b * half : (2 * b + 1) * half, j * QC : (j + 1) * QC] = hi
                lhs2[(2 * b + 1) * half : (2 * b + 2) * half, j * QC : (j + 1) * QC] = lo
            sl = slice(2 * b * half, (2 * b + 2) * half)
            acc[sl, :] += lax.dot_general(
                lhs2[sl, :], rhs2[...], (((1,), (1,)), ((), ())), preferred_element_type=F32
            )
        return carry

    lax.fori_loop(0, nq * steps, step, 0)

    half = pall * 8
    width = block_a * 8
    row_i = lax.rem(lax.broadcasted_iota(jnp.int32, (half, width), 0), 8)
    col_i = lax.rem(lax.broadcasted_iota(jnp.int32, (half, width), 1), 8)
    diag = (row_i == col_i).astype(F32)
    total = jnp.zeros((pall, block_b * block_a), F32)
    src = lax.broadcasted_iota(jnp.int32, (width, block_b * block_a), 0) // 8
    dst = lax.broadcasted_iota(jnp.int32, (width, block_b * block_a), 1)
    for b in range(block_b):
        y = acc[2 * b * half : (2 * b + 1) * half, :] + acc[(2 * b + 1) * half : (2 * b + 2) * half, :]
        y = (y * diag).reshape(pall, 8, width).sum(axis=1)
        pick = (src + b * block_a == dst).astype(F32)
        total += jnp.dot(y, pick, precision=lax.Precision.HIGHEST, preferred_element_type=F32)
    part[...] = total.reshape(no, pairs, block_b * block_a)

    devices = no * nv * na
    me = (occ * nv + vir) * na + aux
    parts[me] = part[occ]

    def final_copy(k):
        j = lax.rem(me + k, devices)
        to = (j // (nv * na), lax.rem(j // na, nv), lax.rem(j, na))
        return pltpu.make_async_remote_copy(
            src_ref=part.at[to[0]],
            dst_ref=parts.at[me],
            send_sem=a_send.at[k],
            recv_sem=a_recv.at[me],
            device_id=to,
            device_id_type=MESH,
        )

    def final_arrival(k):
        j = lax.rem(me + k, devices)
        to = (j // (nv * na), lax.rem(j // na, nv), lax.rem(j, na))
        return pltpu.make_async_remote_copy(
            src_ref=part.at[to[0]],
            dst_ref=parts.at[j],
            send_sem=a_send.at[k],
            recv_sem=a_recv.at[j],
            device_id=to,
            device_id_type=MESH,
        )

    def start_final(k, carry):
        final_copy(k).start()
        return carry

    def wait_final(k, carry):
        final_arrival(k).wait_recv()
        return carry

    def drain_final(k, carry):
        final_copy(k).wait_send()
        return carry

    lax.fori_loop(1, devices, start_final, 0)
    for copy in tau_sends:
        copy.wait_send()
    for n in range(nq):
        for down in (True, False):
            passes = vir > 0 if down else vir < nv - 1

            @pl.when(passes)
            def _():
                right_copy(vir, n, down, True).wait_send()

            for k in waves:
                u = vir + k if down else vir - k
                here = u < nv if down else u >= 0

                @pl.when(passes & here)
                def _():
                    right_copy(u, n, down, False).wait_send()
    lax.fori_loop(1, devices, wait_final, 0)
    out[...] = res[...] + jnp.sum(parts[...], axis=0)
    lax.fori_loop(1, devices, drain_final, 0)


def local(sizes, amplitudes, pair_mask, left_factor, left_mask, right_factor, right_mask, residual_in):
    no, nv, na = sizes
    pairs, cols, virt = amplitudes.shape
    rows, block_b, auxn = right_factor.shape
    block_a = left_factor.shape[0]
    nq = auxn // QC
    depth = rows * nv
    cq = cols // na
    pall = no * pairs
    right = right_factor.reshape(rows, block_b, nq, QC).transpose(2, 0, 1, 3)
    right = right.reshape(nq, rows, block_b * QC)
    ba = block_b * block_a
    vmem = pl.BlockSpec(memory_space=pltpu.VMEM)
    smem = pl.BlockSpec(memory_space=pltpu.SMEM)
    hbm = pl.BlockSpec(memory_space=pltpu.MemorySpace.HBM)
    dma = pltpu.SemaphoreType.DMA
    out = pl.pallas_call(
        functools.partial(kernel, no, nv, na),
        out_shape=jax.ShapeDtypeStruct((pairs, ba), F32),
        in_specs=[smem, smem, smem, hbm, hbm, hbm, vmem],
        out_specs=vmem,
        scratch_shapes=[
            pltpu.VMEM((pairs, cols, virt), BF16),
            pltpu.VMEM(left_factor.shape, BF16),
            pltpu.VMEM((nv, nq, rows, block_b * QC), BF16),
            pltpu.VMEM((depth, block_b * QC), BF16),
            pltpu.VMEM((no, na, pairs, cq, depth), BF16),
            pltpu.VMEM((max(no - 1, 1), pairs, cq, depth), BF16),
            pltpu.VMEM((2 * block_b * pall * 8, CC // 8 * QC), BF16),
            pltpu.VMEM((block_a * 8, CC // 8 * QC), BF16),
            pltpu.VMEM((2 * block_b * pall * 8, block_a * 8), F32),
            pltpu.VMEM((no, pairs, ba), F32),
            pltpu.VMEM((no * nv * na, pairs, ba), F32),
            dma,
            dma((nq,)),
            dma((nq,)),
            dma((2, nv, nq)),
            dma((nv, nq)),
            dma((no, na)),
            dma((no, na)),
            dma((no * nv * na,)),
            dma((no * nv * na,)),
        ],
        compiler_params=pltpu.CompilerParams(
            has_side_effects=True, vmem_limit_bytes=62 * 1024 * 1024
        ),
        name="ladder",
    )(pair_mask, left_mask, right_mask, amplitudes, left_factor, right,
      residual_in.reshape(pairs, ba))
    return out.reshape(pairs, block_b, block_a)


def solution(mesh):
    sizes = tuple(mesh.shape[name] for name in ("occ", "vir", "aux"))
    return jax.shard_map(
        functools.partial(local, sizes),
        mesh=mesh,
        in_specs=(
            P("occ", "vir", None),
            P("occ", "vir", None),
            P(None, "vir", "aux"),
            P("vir", "aux"),
            P(("occ", "vir"), None, "aux"),
            P(None, "aux"),
            P("occ", None, None),
        ),
        out_specs=P("occ", None, None),
        check_vma=False,
    )
```

time: 403 us -> 119 us (0.30); the launches traced: 395 us -> 119 us
  matrix products: 190 us -> 0 us
  Pallas kernels: 0 us -> 113 us
  waiting for transfers between devices: 93.1 us -> 0 us
  blocking collectives: 59.4 us -> 0 us
  other arithmetic: 26.2 us -> 0 us
  between operations: 13.6 us -> 0.01 us
  local copies, waits for them, and re-layouts: 12.5 us -> 5.9 us
    dot_general x9 -> x0, matrix products: 190 us -> none  [the longest x4 142 us: local(): jnp.einsum('pcq,acq->pa', inner_b, left_wide, precision=lax.Precision.HIG...]
    pallas_call x0 -> x1, Pallas kernels: none -> 113 us  [local(): pl.pallas_call(functools.partial(kernel, no, nv, na), out_shape=jax.Shape...]
    all_gather x1 -> x0, waiting for transfers between devices: 93.1 us -> none  [local(): right_whole = lax.all_gather(right, ('occ', 'vir'), axis=0, tiled=True)]
    psum x1 -> x0, blocking collectives: 59.4 us -> none  [local(): total = lax.psum(partial_sum, ('vir', 'aux'))]
    mul x3 -> x0, other arithmetic: 24.7 us -> none  [the longest x1 13.8 us: local(): left_factor * expand_tiles(left_mask, TILE).astype(jnp.bfloat16)[None, :, :]]
    convert_element_type x1 -> x0, local copies, waits for them, and re-layouts: 7.41 us -> none  [local(): tau = amplitudes * expand_tiles(pair_mask, TILE).astype(jnp.bfloat16)]
    reshape x0 -> x4, local copies, waits for them, and re-layouts: none -> 5.9 us  [the longest x1 1.59 us: local(): right = right_factor.reshape(rows, block_b, nq, QC).transpose(2, 0, 1, 3)]
    broadcast_in_dim x4 -> x0, local copies, waits for them, and re-layouts: 4.25 us -> none  [expand_tiles(): return jnp.repeat(jnp.repeat(mask, width, axis=-2), width, axis=-1)]
  transfers between devices with their start and end apart: 1 -> 0, of which waited for: 1 -> 0; matrix products, arithmetic and copies ran while one was open for 9% -> 0% of each run, Pallas kernels for 0% -> 0%
where the time goes in v1:
time: 119 us
  Pallas kernels  113 us (95%)
  local copies, waits for them, and re-layouts  5.9 us (5%)
    pallas_call x1, Pallas kernels, local(): pl.pallas_call(functools.partial(kernel, no, nv, na), out_shape=jax.Shape...  113 us

profile of v1, /device:TPU:0, one launch (start us, length us, event | category | flops | bytes accessed | tf_op | source)
XLA Modules:
  0.0 118.8 jit_solution(8865320359938048704)
XLA Ops:
  0.0 1.6 %copy.11 = bf16[128,1,4,4,256]{4,3,1,0,2:T(4,128)(2,1)S(1)} copy(bf16[128,1,4,4,256]{4,3,2,1,0:T(4,128)(2,1)} %bitcast.8) | data formatting | bytes 2097152 | tf_op jit(solution)/shard_map/reshape | solution.py:335
  1.6 1.6 %reshape.13.right_hbm = bf16[4,128,1024]{2,1,0:T(8,128)(2,1)} reshape(bf16[4,128,4,256]{3,2,1,0:T(4,128)(2,1)S(1)} %bitcast.7) | data formatting | bytes 2097152 | tf_op jit(solution)/shard_map/reshape | solution.py:336
  3.2 1.4 %reshape.14.res = f32[8,128]{1,0:T(8,128)} reshape(f32[8,4,32]{2,1,0:T(4,128)} %param.13) | data formatting | bytes 8192 | tf_op jit(solution)/shard_map/reshape | solution.py:374
  4.5 112.9 %ladder.1 = f32[8,128]{1,0:T(8,128)} custom-call(s32[8,2,8]{2,1,0:T(2,128)} %pair_mask.1, s32[2,8]{1,0:T(2,128)} %left_mask.1, s32[8,8]{1,0:T(8,128)} %right_mask.1, bf16[8,256,1024]{2,1,0:T(8,128)(2,1)} %amp_hbm.1, bf16[32,256,1024]{2,1,0:T(8,128)(2,1)} %left_hbm.1, bf16[4,128,1024]{2,1,0:T(8,128)(2,1)} %reshape.13.right_hbm, f32[8,128]{1,0:T(8,128)} %reshape.14.res), custom_call_target="tpu_custom_call" | custom-call | tf_op jit(solution)/shard_map/ladder/pallas_call | solution.py:342
  117.4 1.4 %reshape.15 = f32[8,4,32]{2,1,0:T(4,128)} reshape(f32[8,128]{1,0:T(8,128)} %ladder.1) | data formatting | bytes 8192 | tf_op jit(solution)/shard_map/reshape | solution.py:375
